TPU v7x, 32 devices: a whole 2x2x4 slice. The times are simulated.
32 devices in a mesh: gx: 8 (over y, x, core), gy: 4 (over z).
Axes of the slice: x: 2, y: 2, z: 4, core: 2. Of those that a mesh axis runs over, the one named last changes fastest.
Arguments:
- eastward: float32 [64, 512, 128], P('gx', 'gy'), may hold values from -6 to 6
- northward: float32 [64, 512, 128], P('gx', 'gy'), may hold values from -6 to 6
- vertical: float32 [64, 512, 128], P('gx', 'gy'), may hold values from -6 to 6
- pressure: float32 [64, 512, 128], P('gx', 'gy'), may hold values from -6 to 6
- theta: float32 [64, 512, 128], P('gx', 'gy'), may hold values from -6 to 6
- humidity: float32 [64, 512, 128], P('gx', 'gy'), may hold values from 0.95 to 1.07
- sound_speed: float32 [128], replicated, may hold values from 0.25 to 1
- radius_sq: float32 [64, 8, 64, 512], P(None, None, 'gx', 'gy'), may hold values from 0.25 to 4
- multiplicity: bfloat16 [64, 8, 64, 512], P(None, None, 'gx', 'gy'), may hold values from 0.5 to 2
- droplet_count: int32 [8, 64, 512], P(None, 'gx', 'gy'), may hold values from 0 to 64
Outputs:
- eastward_out: float32 [64, 512, 128], P('gx', 'gy')
- northward_out: float32 [64, 512, 128], P('gx', 'gy')
- vertical_out: float32 [64, 512, 128], P('gx', 'gy')
- pressure_out: float32 [64, 512, 128], P('gx', 'gy')
- theta_out: float32 [64, 512, 128], P('gx', 'gy')
- humidity_out: float32 [64, 512, 128], P('gx', 'gy')
- radius_out: float32 [64, 8, 64, 512], P(None, None, 'gx', 'gy')
- saturation_profile: float32 [128], replicated
All inputs are finite; a program needn't handle non-finite values.
Results may differ from a plain program's by a relative error of at most 0.0003.
Values sent between devices are 32-bit elements; how exact they have to be, the bound alone decides.
No kernel may reach another device: no remote copies, remote signals or barrier semaphores. Data moves between devices by JAX's collectives and lax.ppermute only.
A program may use at most 64 MiB of HBM per device.

v0:
```python
import jax
import jax.numpy as jnp
from jax import lax
from jax.sharding import PartitionSpec as P

SUB = 3
TIME_STEP = 1.0
BUOYANCY = 0.5
VAPOUR_SLOPE = 0.01
GROWTH_RATE = 25.0
RADIUS_FLOOR = 0.0625
MASS_FACTOR = 0.0004
LATENT_HEAT = 200.0


def padded_2(value, sides, width):
    for axis, dim in sides:
        count, length = (lax.axis_size(axis), value.shape[dim])
        up = [(i, (i + 1) % count) for i in range(count)]
        down = [(j, i) for i, j in up]
        last = lax.slice_in_dim(value, length - width, length, axis=dim)
        initial = lax.slice_in_dim(value, 0, width, axis=dim)
        before = lax.ppermute(last, axis, up)
        after = lax.ppermute(initial, axis, down)
        value = jnp.concatenate([before, value, after], axis=dim)
    return value


def column_tables(sound_speed):
    levels = sound_speed.shape[0]
    rows = lax.broadcasted_iota(jnp.int32, (levels, levels), 0)
    cols = lax.broadcasted_iota(jnp.int32, (levels, levels), 1)
    inside = rows < levels - 1
    gradient = jnp.where(inside & (cols == rows + 1), 1.0, 0.0) - jnp.where(
        inside & (cols == rows), 1.0, 0.0
    )
    gradient = gradient.astype(jnp.float32)
    scaled = gradient * sound_speed[None, :]
    product = jnp.dot(
        scaled, gradient.T, precision=lax.Precision.HIGHEST, preferred_element_type=jnp.float32
    )
    matrix = jnp.eye(levels, dtype=jnp.float32) + TIME_STEP * TIME_STEP * product
    factor = jnp.linalg.cholesky(matrix)
    identity = jnp.eye(levels, dtype=jnp.float32)
    halfway = lax.linalg.triangular_solve(factor, identity, left_side=True, lower=True)
    inverse = lax.linalg.triangular_solve(
        factor, halfway, left_side=True, lower=True, transpose_a=True
    )
    lifted = TIME_STEP * jnp.dot(
        gradient.T, inverse, precision=lax.Precision.HIGHEST, preferred_element_type=jnp.float32
    )
    return (inverse, lifted, gradient)


def column_update(pressure, vertical, heat, divergence, sound_speed, tables):
    inverse, lifted, gradient = tables
    levels = pressure.shape[-1]
    interior = (lax.broadcasted_iota(jnp.int32, (levels,), 0) < levels - 1).astype(jnp.float32)
    explicit = pressure - TIME_STEP * sound_speed * divergence
    forcing = (interior * (vertical + TIME_STEP * BUOYANCY * heat)).reshape(-1, levels)
    flat_explicit = explicit.reshape(-1, levels)
    solved = jnp.dot(
        forcing, inverse, precision=lax.Precision.HIGHEST, preferred_element_type=jnp.float32
    )
    solved = solved - jnp.dot(
        flat_explicit, lifted, precision=lax.Precision.HIGHEST, preferred_element_type=jnp.float32
    )
    stepped = jnp.dot(
        solved, gradient, precision=lax.Precision.HIGHEST, preferred_element_type=jnp.float32
    )
    new_pressure = flat_explicit + TIME_STEP * sound_speed * stepped
    return (new_pressure.reshape(explicit.shape), solved.reshape(explicit.shape))


def horizontal_velocity(eastward, northward, padded):
    grad_east = (padded[2:, 1:-1] - padded[:-2, 1:-1]) * 0.5
    grad_north = (padded[1:-1, 2:] - padded[1:-1, :-2]) * 0.5
    return (eastward - TIME_STEP * grad_east, northward - TIME_STEP * grad_north)


def horizontal_spread(east_padded, north_padded):
    return (
        east_padded[2:, 1:-1]
        - east_padded[:-2, 1:-1]
        + north_padded[1:-1, 2:]
        - north_padded[1:-1, :-2]
    ) * 0.5


def condense(theta, humidity, radius_sq, multiplicity, droplet_count):
    levels = theta.shape[2]
    layers = radius_sq.shape[1]
    lowest = levels // 4
    sat = humidity * jnp.exp(-VAPOUR_SLOPE * theta) - 1.0
    cloud = jnp.transpose(sat[:, :, lowest : lowest + layers], (2, 0, 1))
    grown = jnp.maximum(radius_sq + GROWTH_RATE * cloud[None], RADIUS_FLOOR)
    live = lax.broadcasted_iota(jnp.int32, radius_sq.shape, 0) < droplet_count[None]
    mass = multiplicity.astype(jnp.float32) * (
        grown * jnp.sqrt(grown) - radius_sq * jnp.sqrt(radius_sq)
    )
    change = MASS_FACTOR * jnp.sum(jnp.where(live, mass, 0.0), axis=0)
    added = jnp.pad(
        jnp.transpose(change, (1, 2, 0)), ((0, 0), (0, 0), (lowest, levels - lowest - layers))
    )
    humidity_out = humidity - added
    theta_out = theta + LATENT_HEAT * added
    radius_out = jnp.where(live, grown, 0.0)
    percent = 100.0 * (humidity_out * jnp.exp(-VAPOUR_SLOPE * theta_out) - 1.0)
    return (humidity_out, theta_out, radius_out, percent)


def level_means(percent, theta_out, columns):
    totals = lax.psum(
        (jnp.sum(percent, axis=(0, 1)), jnp.sum(theta_out, axis=(0, 1))), ("gx", "gy")
    )
    return (totals[0] / columns, totals[1] / columns)


def local(
    eastward,
    northward,
    vertical,
    pressure,
    theta,
    humidity,
    sound_speed,
    radius_sq,
    multiplicity,
    droplet_count,
):
    humidity_out, theta_out, radius_out, percent = condense(
        theta, humidity, radius_sq, multiplicity, droplet_count
    )
    columns = float(theta.shape[0] * theta.shape[1] * lax.axis_size("gx") * lax.axis_size("gy"))
    tables = column_tables(sound_speed)
    saturation_profile, theta_mean = level_means(percent, theta_out, columns)
    heat = theta_out - theta_mean
    margin = 2 * SUB
    eastward, northward, vertical, pressure, heating = (
        padded_2(eastward, (("gx", 0), ("gy", 1)), margin),
        padded_2(northward, (("gx", 0), ("gy", 1)), margin),
        padded_2(vertical, (("gx", 0), ("gy", 1)), margin),
        padded_2(pressure, (("gx", 0), ("gy", 1)), margin),
        padded_2(heat, (("gx", 0), ("gy", 1)), margin),
    )
    for substep in range(SUB):
        east_new, north_new = horizontal_velocity(
            eastward[1:-1, 1:-1], northward[1:-1, 1:-1], pressure
        )
        spread = horizontal_spread(east_new, north_new)
        heating = heating[2:-2, 2:-2]
        pressure, vertical = column_update(
            pressure[2:-2, 2:-2], vertical[2:-2, 2:-2], heating, spread, sound_speed, tables
        )
        eastward, northward = (east_new[1:-1, 1:-1], north_new[1:-1, 1:-1])
    return (
        eastward,
        northward,
        vertical,
        pressure,
        theta_out,
        humidity_out,
        radius_out,
        saturation_profile,
    )


def solution(mesh):
    return jax.shard_map(
        local,
        mesh=mesh,
        in_specs=(
            P("gx", "gy", None),
            P("gx", "gy", None),
            P("gx", "gy", None),
            P("gx", "gy", None),
            P("gx", "gy", None),
            P("gx", "gy", None),
            P(),
            P(None, None, "gx", "gy"),
            P(None, None, "gx", "gy"),
            P(None, "gx", "gy"),
        ),
        out_specs=(
            P("gx", "gy", None),
            P("gx", "gy", None),
            P("gx", "gy", None),
            P("gx", "gy", None),
            P("gx", "gy", None),
            P("gx", "gy", None),
            P(None, None, "gx", "gy"),
            P(),
        ),
        check_vma=False,
    )
```

profile of v0, /device:TPU:0, one launch (start us, length us, event | category | flops | bytes accessed | tf_op | source)
XLA Modules:
  0.0 179.3 jit_solution(16261416911662587209)
XLA Ops:
  0.7 2.1 %fusion.102 = (f32[6,128,128]{2,1,0:T(8,128)}, f32[6,128,128]{2,1,0:T(8,128)}) fusion(f32[8,128,128]{2,1,0:T(8,128)} %param.13), kind=kLoop, calls=%fused_computation.159 | loop fusion | bytes 1572864 | tf_op jit(solution)/shard_map/slice | solution.py:22
  3.3 2.9 %collective-permute-start.5 = (f32[6,128,128]{2,1,0:T(8,128)}, f32[6,128,128]{2,1,0:T(8,128)}, u32[]{:S(2)}, u32[]{:S(2)}) collective-permute-start(f32[6,128,128]{2,1,0:T(8,128)} %get-tuple-element.67), channel_id=1, source_target_pairs={{4,0},{8,4},{12,8},{16,12},{20,16},{24,20},{28,24},{0,28},{5,1},{9... | collective-permute-start | bytes 1179656 | tf_op jit(solution)/shard_map/ppermute | solution.py:24
  7.2 2.6 %collective-permute-start.1 = (f32[6,128,128]{2,1,0:T(8,128)}, f32[6,128,128]{2,1,0:T(8,128)}, u32[]{:S(2)}, u32[]{:S(2)}) collective-permute-start(f32[6,128,128]{2,1,0:T(8,128)} %get-tuple-element.63), channel_id=1, source_target_pairs={{4,0},{8,4},{12,8},{16,12},{20,16},{24,20},{28,24},{0,28},{5,1},{9... | collective-permute-start | bytes 1179656 | tf_op jit(solution)/shard_map/ppermute | solution.py:24
  11.5 4.9 %fusion.6 = (f32[64,8,8,128]{3,2,1,0:T(8,128)}, f32[8,8,128]{2,1,0:T(8,128)S(1)}) fusion(f32[64,8,8,128]{3,2,1,0:T(8,128)} %param.17, f32[8,8,128]{2,1,0:T(8,128)S(1)} %fusion.58, s32[8,8,128]{2,1,0:T(8,128)S(1)} %copy-done.26, bf16[64,8,8,128]{3,2,1,0:T(8,128)(2,1)} %param.18), kind=kLoop, calls=%fused_computation.13 | loop fusion | flops 5758976 | bytes 5341184 | tf_op jit(solution)/shard_map/jit(_where)/select_n | solution.py:107
  17.4 44.2 %all-reduce.1 = (f32[128]{0:T(128)S(1)}, f32[128]{0:T(128)S(1)}) all-reduce(f32[128]{0:T(128)S(1)} %get-tuple-element.33, f32[128]{0:T(128)S(1)} %get-tuple-element.32), channel_id=1, replica_groups=mesh['gx'=8,'gy'=4] {'gx','gy'}, use_global_device_ids=true, to_apply=%region_2.3 | all-reduce | flops 256 | bytes 2048 | tf_op jit(solution)/shard_map/psum | solution.py:113
  63.8 11.7 %cholesky.17 = f32[128,128]{1,0:T(8,128)S(1)} custom-call(f32[128,128]{1,0:T(8,128)S(1)} %fusion.42), custom_call_target="Cholesky" | custom-call | tf_op jit(solution)/shard_map/jit(cholesky)/cholesky | solution.py:43
  76.9 9.8 %custom-call.8 = f32[1,128,128]{1,2,0:T(8,128)S(1)} custom-call(f32[1,128,128]{2,1,0:T(8,128)S(1)} %fusion.36), custom_call_target="InvertDiagBlocksLowerTriangular" | custom-call | tf_op jit(solution)/shard_map/triangular_solve | solution.py:46
  94.3 2.7 %collective-permute-start.9 = (f32[6,128,128]{2,1,0:T(8,128)}, f32[6,128,128]{2,1,0:T(8,128)}, u32[]{:S(2)}, u32[]{:S(2)}) collective-permute-start(f32[6,128,128]{2,1,0:T(8,128)} %get-tuple-element.65), channel_id=1, source_target_pairs={{4,0},{8,4},{12,8},{16,12},{20,16},{24,20},{28,24},{0,28},{5,1},{9... | collective-permute-start | bytes 1179656 | tf_op jit(solution)/shard_map/ppermute | solution.py:24
  98.1 4.5 %collective-permute-done.17 = f32[6,128,128]{1,0,2:T(8,128)S(1)} collective-permute-done((f32[6,128,128]{1,0,2:T(8,128)S(1)}, f32[6,128,128]{1,0,2:T(8,128)S(1)}, u32[]{:S(2)}, u32[]{:S(2)}) %collective-permute-start.17) | collective-permute-done | bytes 393248 | tf_op jit(solution)/shard_map/ppermute | solution.py:24
  102.5 2.8 %collective-permute-start.13 = (f32[6,128,128]{2,0,1:T(8,128)}, f32[6,128,128]{2,0,1:T(8,128)}, u32[]{:S(2)}, u32[]{:S(2)}) collective-permute-start(f32[6,128,128]{2,0,1:T(8,128)} %get-tuple-element.60), channel_id=1, source_target_pairs={{4,0},{8,4},{12,8},{16,12},{20,16},{24,20},{28,24},{0,28},{5,1},{9... | collective-permute-start | bytes 1179656 | tf_op jit(solution)/shard_map/ppermute | solution.py:24
  105.3 3.0 %collective-permute-done.16 = f32[6,128,128]{1,0,2:T(8,128)S(1)} collective-permute-done((f32[6,128,128]{1,0,2:T(8,128)S(1)}, f32[6,128,128]{1,0,2:T(8,128)S(1)}, u32[]{:S(2)}, u32[]{:S(2)}) %collective-permute-start.16) | collective-permute-done | bytes 393248 | tf_op jit(solution)/shard_map/ppermute | solution.py:23
  108.6 1.6 collective-permute-start.7
  111.2 2.1 %fusion.94 = (f32[20,6,128]{1,0,2:T(8,128)}, f32[20,6,128]{1,0,2:T(8,128)}) fusion(f32[20,128,128]{1,0,2:T(8,128)S(1)} %pad_maximum_fusion.1), kind=kLoop, calls=%fused_computation.151 | loop fusion | bytes 245760 | tf_op jit(solution)/shard_map/slice | solution.py:21
  117.0 1.9 %copy.56 = f32[20,6,128]{2,0,1:T(8,128)S(1)} copy(f32[20,6,128]{1,0,2:T(8,128)} %get-tuple-element.43) | data formatting | bytes 122880 | tf_op jit(solution)/shard_map/slice | solution.py:22
  118.9 1.9 %copy.55 = f32[20,6,128]{2,0,1:T(8,128)S(1)} copy(f32[20,6,128]{1,0,2:T(8,128)} %get-tuple-element.42) | data formatting | bytes 122880 | tf_op jit(solution)/shard_map/slice | solution.py:21
  120.8 3.4 %collective-permute-start.3 = (f32[20,6,128]{2,1,0:T(8,128)S(1)}, f32[20,6,128]{2,1,0:T(8,128)S(1)}, u32[]{:S(2)}, u32[]{:S(2)}) collective-permute-start(f32[20,6,128]{2,1,0:T(8,128)S(1)} %get-tuple-element.47), channel_id=1, source_target_pairs={{1,0},{2,1},{3,2},{0,3},{5,4},{6,5},{7,6},{4,7},{9,8},{10,9},{11,1... | collective-permute-start | bytes 184328 | tf_op jit(solution)/shard_map/ppermute | solution.py:24
  124.2 1.8 constant_dynamic-update-slice_fusion.6
  127.0 2.0 %collective-permute-start.18 = (f32[20,6,128]{2,0,1:T(8,128)S(1)}, f32[20,6,128]{2,0,1:T(8,128)S(1)}, u32[]{:S(2)}, u32[]{:S(2)}) collective-permute-start(f32[20,6,128]{2,0,1:T(8,128)S(1)} %copy.55), channel_id=1, source_target_pairs={{0,1},{1,2},{2,3},{3,0},{4,5},{5,6},{6,7},{7,4},{8,9},{9,10},{10,1... | collective-permute-start | bytes 184328 | tf_op jit(solution)/shard_map/ppermute | solution.py:23
  131.6 1.5 copy.58
  133.1 1.8 copy.50
  134.9 2.1 %collective-permute-start.15 = (f32[20,6,128]{2,0,1:T(8,128)S(1)}, f32[20,6,128]{2,0,1:T(8,128)S(1)}, u32[]{:S(2)}, u32[]{:S(2)}) collective-permute-start(f32[20,6,128]{2,0,1:T(8,128)S(1)} %get-tuple-element.41), channel_id=1, source_target_pairs={{1,0},{2,1},{3,2},{0,3},{5,4},{6,5},{7,6},{4,7},{9,8},{10,9},{11,1... | collective-permute-start | bytes 184328 | tf_op jit(solution)/shard_map/ppermute | solution.py:24
  137.3 2.4 %collective-permute-done.15 = f32[20,6,128]{2,0,1:T(8,128)S(1)} collective-permute-done((f32[20,6,128]{2,0,1:T(8,128)S(1)}, f32[20,6,128]{2,0,1:T(8,128)S(1)}, u32[]{:S(2)}, u32[]{:S(2)}) %collective-permute-start.15) | collective-permute-done | bytes 61472 | tf_op jit(solution)/shard_map/ppermute | solution.py:24
  139.7 4.5 %collective-permute-done.14 = f32[20,6,128]{2,0,1:T(8,128)S(1)} collective-permute-done((f32[20,6,128]{2,0,1:T(8,128)S(1)}, f32[20,6,128]{2,0,1:T(8,128)S(1)}, u32[]{:S(2)}, u32[]{:S(2)}) %collective-permute-start.14) | collective-permute-done | bytes 61472 | tf_op jit(solution)/shard_map/ppermute | solution.py:23
  145.6 2.1 %collective-permute-start.10 = (f32[20,6,128]{2,1,0:T(8,128)S(1)}, f32[20,6,128]{2,1,0:T(8,128)S(1)}, u32[]{:S(2)}, u32[]{:S(2)}) collective-permute-start(f32[20,6,128]{2,1,0:T(8,128)S(1)} %get-tuple-element.48), channel_id=1, source_target_pairs={{0,1},{1,2},{2,3},{3,0},{4,5},{5,6},{6,7},{7,4},{8,9},{9,10},{10,1... | collective-permute-start | bytes 184328 | tf_op jit(solution)/shard_map/ppermute | solution.py:23
  149.1 2.8 %collective-permute-done.10 = f32[20,6,128]{2,1,0:T(8,128)S(1)} collective-permute-done((f32[20,6,128]{2,1,0:T(8,128)S(1)}, f32[20,6,128]{2,1,0:T(8,128)S(1)}, u32[]{:S(2)}, u32[]{:S(2)}) %collective-permute-start.10) | collective-permute-done | bytes 61472 | tf_op jit(solution)/shard_map/ppermute | solution.py:23
  157.0 2.1 %reshape.77 = f32[1584,128]{1,0:T(8,128)} reshape(f32[12,132,128]{2,1,0:T(8,128)} %fusion.23) | data formatting | bytes 1622016 | tf_op jit(solution)/shard_map/reshape | solution.py:61
  159.1 2.3 %fusion.21 = f32[12,132,128]{2,1,0:T(8,128)} fusion(f32[20,140,128]{2,1,0:T(8,128)} %copy-done.2, f32[16,136,128]{2,1,0:T(8,128)S(1)} %bitcast.50, f32[128]{0:T(128)S(1)} %fusion.81), kind=kLoop, calls=%fused_computation.50 | loop fusion | flops 608256 | bytes 2433536 | tf_op jit(solution)/shard_map/mul | solution.py:60
  161.3 2.2 %reshape.79 = f32[1584,128]{1,0:T(8,128)} reshape(f32[12,132,128]{2,1,0:T(8,128)} %fusion.21) | data formatting | bytes 1622016 | tf_op jit(solution)/shard_map/reshape | solution.py:60
  163.5 1.9 %fusion.104 = f32[1584,128]{1,0:T(8,128)S(1)} fusion(f32[1584,128]{1,0:T(8,128)} %reshape.79, f32[128,128]{1,0:T(8,128)S(1)} %fusion.37), kind=kOutput, calls=%fused_computation.161 | convolution fusion | flops 311427072 | bytes 1687552 | tf_op jit(solution)/shard_map/dot_general | solution.py:62
  167.2 1.8 fusion.1
  169.0 2.1 %reshape.81 = f32[12,132,128]{2,1,0:T(8,128)} reshape(f32[1584,128]{1,0:T(8,128)} %copy-done.5) | data formatting | bytes 1622016 | tf_op jit(solution)/shard_map/reshape | solution.py:72
  177.8 1.5 fusion.11
  (162 shorter events, 41.2 us)
Async XLA Ops:
  0.6 9.2 %copy-start.10 = (f32[8,128,128]{2,1,0:T(8,128)S(1)}, f32[8,128,128]{2,1,0:T(8,128)}, u32[]{:S(2)}) copy-start(f32[8,128,128]{2,1,0:T(8,128)} %param.11) | copy-start | bytes 1572868
  2.8 88.2 %collective-permute-start.4 = (f32[6,128,128]{2,1,0:T(8,128)}, f32[6,128,128]{2,1,0:T(8,128)}, u32[]{:S(2)}, u32[]{:S(2)}) collective-permute-start(f32[6,128,128]{2,1,0:T(8,128)} %get-tuple-element.68), channel_id=1, source_target_pairs={{0,4},{4,8},{8,12},{12,16},{16,20},{20,24},{24,28},{28,0},{1,5},{5... | collective-permute-start | bytes 1179656 | tf_op jit(solution)/shard_map/ppermute | solution.py:23
  3.3 7.5 %copy-start.21 = (f32[8,128,128]{2,1,0:T(8,128)S(1)}, f32[8,128,128]{2,1,0:T(8,128)}, u32[]{:S(2)}) copy-start(f32[8,128,128]{2,1,0:T(8,128)} %param.15) | copy-start | bytes 1572868
  3.3 91.0 %collective-permute-start.5 = (f32[6,128,128]{2,1,0:T(8,128)}, f32[6,128,128]{2,1,0:T(8,128)}, u32[]{:S(2)}, u32[]{:S(2)}) collective-permute-start(f32[6,128,128]{2,1,0:T(8,128)} %get-tuple-element.67), channel_id=1, source_target_pairs={{4,0},{8,4},{12,8},{16,12},{20,16},{24,20},{28,24},{0,28},{5,1},{9... | collective-permute-start | bytes 1179656 | tf_op jit(solution)/shard_map/ppermute | solution.py:24
  7.2 86.0 %collective-permute-start = (f32[6,128,128]{2,1,0:T(8,128)}, f32[6,128,128]{2,1,0:T(8,128)}, u32[]{:S(2)}, u32[]{:S(2)}) collective-permute-start(f32[6,128,128]{2,1,0:T(8,128)} %get-tuple-element.64), channel_id=1, source_target_pairs={{0,4},{4,8},{8,12},{12,16},{16,20},{20,24},{24,28},{28,0},{1,5},{5... | collective-permute-start | bytes 1179656 | tf_op jit(solution)/shard_map/ppermute | solution.py:23
  7.2 106.2 %collective-permute-start.1 = (f32[6,128,128]{2,1,0:T(8,128)}, f32[6,128,128]{2,1,0:T(8,128)}, u32[]{:S(2)}, u32[]{:S(2)}) collective-permute-start(f32[6,128,128]{2,1,0:T(8,128)} %get-tuple-element.63), channel_id=1, source_target_pairs={{4,0},{8,4},{12,8},{16,12},{20,16},{24,20},{28,24},{0,28},{5,1},{9... | collective-permute-start | bytes 1179656 | tf_op jit(solution)/shard_map/ppermute | solution.py:24
  10.8 97.8 %collective-permute-start.8 = (f32[6,128,128]{2,1,0:T(8,128)}, f32[6,128,128]{2,1,0:T(8,128)}, u32[]{:S(2)}, u32[]{:S(2)}) collective-permute-start(f32[6,128,128]{2,1,0:T(8,128)} %get-tuple-element.66), channel_id=1, source_target_pairs={{0,4},{4,8},{8,12},{12,16},{16,20},{20,24},{24,28},{28,0},{1,5},{5... | collective-permute-start | bytes 1179656 | tf_op jit(solution)/shard_map/ppermute | solution.py:23
  10.8 155.5 %copy-start.28 = (s32[128]{0:T(128)}, s32[128]{0:T(128)S(1)}, u32[]{:S(2)}) copy-start(s32[128]{0:T(128)S(1)} %iota_add_fusion) | copy-start | bytes 1540
  10.8 155.5 %copy-start.30 = (pred[128]{0:T(512)(128)(4,1)}, pred[128]{0:T(512)(128)(4,1)S(1)}, u32[]{:S(2)}) copy-start(pred[128]{0:T(512)(128)(4,1)S(1)} %iota_compare_fusion.6) | copy-start | bytes 388
  17.4 70.1 %copy-start = (f32[8,128,128]{1,0,2:T(8,128)}, f32[8,128,128]{1,0,2:T(8,128)S(1)}, u32[]{:S(2)}) copy-start(f32[8,128,128]{1,0,2:T(8,128)S(1)} %get-tuple-element.37) | copy-start | bytes 1572868
  63.4 25.2 %copy-start.23 = (f32[8,128,128]{2,1,0:T(8,128)S(1)}, f32[8,128,128]{2,1,0:T(8,128)}, u32[]{:S(2)}) copy-start(f32[8,128,128]{2,1,0:T(8,128)} %param.12) | copy-start | bytes 1572868
  87.5 77.9 %copy-start.19 = (f32[128,128]{1,0:T(8,128)}, f32[128,128]{1,0:T(8,128)S(1)}, u32[]{:S(2)}) copy-start(f32[128,128]{1,0:T(8,128)S(1)} %fusion.44) | copy-start | bytes 196612
  87.6 68.1 %copy-start.34 = (f32[128]{0:T(128)}, f32[128]{0:T(128)S(1)}, u32[]{:S(2)}) copy-start(f32[128]{0:T(128)S(1)} %broadcast_multiply_fusion.2) | copy-start | bytes 1540
  87.6 71.5 %copy-start.32 = (f32[128]{0:T(128)}, f32[128]{0:T(128)S(1)}, u32[]{:S(2)}) copy-start(f32[128]{0:T(128)S(1)} %fusion.81) | copy-start | bytes 1540
  91.2 11.3 %collective-permute-start.17 = (f32[6,128,128]{1,0,2:T(8,128)S(1)}, f32[6,128,128]{1,0,2:T(8,128)S(1)}, u32[]{:S(2)}, u32[]{:S(2)}) collective-permute-start(f32[6,128,128]{1,0,2:T(8,128)S(1)} %copy-done.25), channel_id=1, source_target_pairs={{4,0},{8,4},{12,8},{16,12},{20,16},{24,20},{28,24},{0,28},{5,1},{9... | collective-permute-start | bytes 1179656 | tf_op jit(solution)/shard_map/ppermute | solution.py:24
  93.1 15.2 %collective-permute-start.16 = (f32[6,128,128]{1,0,2:T(8,128)S(1)}, f32[6,128,128]{1,0,2:T(8,128)S(1)}, u32[]{:S(2)}, u32[]{:S(2)}) collective-permute-start(f32[6,128,128]{1,0,2:T(8,128)S(1)} %copy-done.24), channel_id=1, source_target_pairs={{0,4},{4,8},{8,12},{12,16},{16,20},{20,24},{24,28},{28,0},{1,5},{5... | collective-permute-start | bytes 1179656 | tf_op jit(solution)/shard_map/ppermute | solution.py:23
  94.3 26.5 %collective-permute-start.9 = (f32[6,128,128]{2,1,0:T(8,128)}, f32[6,128,128]{2,1,0:T(8,128)}, u32[]{:S(2)}, u32[]{:S(2)}) collective-permute-start(f32[6,128,128]{2,1,0:T(8,128)} %get-tuple-element.65), channel_id=1, source_target_pairs={{4,0},{8,4},{12,8},{16,12},{20,16},{24,20},{28,24},{0,28},{5,1},{9... | collective-permute-start | bytes 1179656 | tf_op jit(solution)/shard_map/ppermute | solution.py:24
  98.1 10.5 %copy-start.11 = (f32[20,128,128]{2,1,0:T(8,128)}, f32[20,128,128]{2,1,0:T(8,128)S(1)}, u32[]{:S(2)}) copy-start(f32[20,128,128]{2,1,0:T(8,128)S(1)} %constant_dynamic-update-slice_fusion.3) | copy-start | bytes 3932164
  102.5 24.4 %collective-permute-start.13 = (f32[6,128,128]{2,0,1:T(8,128)}, f32[6,128,128]{2,0,1:T(8,128)}, u32[]{:S(2)}, u32[]{:S(2)}) collective-permute-start(f32[6,128,128]{2,0,1:T(8,128)} %get-tuple-element.60), channel_id=1, source_target_pairs={{4,0},{8,4},{12,8},{16,12},{20,16},{24,20},{28,24},{0,28},{5,1},{9... | collective-permute-start | bytes 1179656 | tf_op jit(solution)/shard_map/ppermute | solution.py:24
  108.3 18.7 %collective-permute-start.12 = (f32[6,128,128]{2,0,1:T(8,128)}, f32[6,128,128]{2,0,1:T(8,128)}, u32[]{:S(2)}, u32[]{:S(2)}) collective-permute-start(f32[6,128,128]{2,0,1:T(8,128)} %get-tuple-element.59), channel_id=1, source_target_pairs={{0,4},{4,8},{8,12},{12,16},{16,20},{20,24},{24,28},{28,0},{1,5},{5... | collective-permute-start | bytes 1179656 | tf_op jit(solution)/shard_map/ppermute | solution.py:23
  108.6 37.0 %collective-permute-start.7 = (f32[20,6,128]{2,1,0:T(8,128)S(1)}, f32[20,6,128]{2,1,0:T(8,128)S(1)}, u32[]{:S(2)}, u32[]{:S(2)}) collective-permute-start(f32[20,6,128]{2,1,0:T(8,128)S(1)} %get-tuple-element.51), channel_id=1, source_target_pairs={{1,0},{2,1},{3,2},{0,3},{5,4},{6,5},{7,6},{4,7},{9,8},{10,9},{11,1... | collective-permute-start | bytes 184328 | tf_op jit(solution)/shard_map/ppermute | solution.py:24
  113.3 34.3 %collective-permute-start.6 = (f32[20,6,128]{2,1,0:T(8,128)S(1)}, f32[20,6,128]{2,1,0:T(8,128)S(1)}, u32[]{:S(2)}, u32[]{:S(2)}) collective-permute-start(f32[20,6,128]{2,1,0:T(8,128)S(1)} %get-tuple-element.50), channel_id=1, source_target_pairs={{0,1},{1,2},{2,3},{3,0},{4,5},{5,6},{6,7},{7,4},{8,9},{9,10},{10,1... | collective-permute-start | bytes 184328 | tf_op jit(solution)/shard_map/ppermute | solution.py:23
  120.8 27.0 %collective-permute-start.3 = (f32[20,6,128]{2,1,0:T(8,128)S(1)}, f32[20,6,128]{2,1,0:T(8,128)S(1)}, u32[]{:S(2)}, u32[]{:S(2)}) collective-permute-start(f32[20,6,128]{2,1,0:T(8,128)S(1)} %get-tuple-element.47), channel_id=1, source_target_pairs={{1,0},{2,1},{3,2},{0,3},{5,4},{6,5},{7,6},{4,7},{9,8},{10,9},{11,1... | collective-permute-start | bytes 184328 | tf_op jit(solution)/shard_map/ppermute | solution.py:24
  126.9 8.0 %collective-permute-start.19 = (f32[20,6,128]{2,0,1:T(8,128)S(1)}, f32[20,6,128]{2,0,1:T(8,128)S(1)}, u32[]{:S(2)}, u32[]{:S(2)}) collective-permute-start(f32[20,6,128]{2,0,1:T(8,128)S(1)} %copy.56), channel_id=1, source_target_pairs={{1,0},{2,1},{3,2},{0,3},{5,4},{6,5},{7,6},{4,7},{9,8},{10,9},{11,1... | collective-permute-start | bytes 184328 | tf_op jit(solution)/shard_map/ppermute | solution.py:24
  127.0 10.1 %collective-permute-start.18 = (f32[20,6,128]{2,0,1:T(8,128)S(1)}, f32[20,6,128]{2,0,1:T(8,128)S(1)}, u32[]{:S(2)}, u32[]{:S(2)}) collective-permute-start(f32[20,6,128]{2,0,1:T(8,128)S(1)} %copy.55), channel_id=1, source_target_pairs={{0,1},{1,2},{2,3},{3,0},{4,5},{5,6},{6,7},{7,4},{8,9},{9,10},{10,1... | collective-permute-start | bytes 184328 | tf_op jit(solution)/shard_map/ppermute | solution.py:23
  134.9 4.8 %collective-permute-start.15 = (f32[20,6,128]{2,0,1:T(8,128)S(1)}, f32[20,6,128]{2,0,1:T(8,128)S(1)}, u32[]{:S(2)}, u32[]{:S(2)}) collective-permute-start(f32[20,6,128]{2,0,1:T(8,128)S(1)} %get-tuple-element.41), channel_id=1, source_target_pairs={{1,0},{2,1},{3,2},{0,3},{5,4},{6,5},{7,6},{4,7},{9,8},{10,9},{11,1... | collective-permute-start | bytes 184328 | tf_op jit(solution)/shard_map/ppermute | solution.py:24
  137.1 7.1 %collective-permute-start.14 = (f32[20,6,128]{2,0,1:T(8,128)S(1)}, f32[20,6,128]{2,0,1:T(8,128)S(1)}, u32[]{:S(2)}, u32[]{:S(2)}) collective-permute-start(f32[20,6,128]{2,0,1:T(8,128)S(1)} %get-tuple-element.40), channel_id=1, source_target_pairs={{0,1},{1,2},{2,3},{3,0},{4,5},{5,6},{6,7},{7,4},{8,9},{9,10},{10,1... | collective-permute-start | bytes 184328 | tf_op jit(solution)/shard_map/ppermute | solution.py:23
  137.3 7.2 %copy-start.2 = (f32[20,140,128]{2,1,0:T(8,128)}, f32[20,140,128]{2,1,0:T(8,128)S(1)}, u32[]{:S(2)}) copy-start(f32[20,140,128]{2,1,0:T(8,128)S(1)} %pad_maximum_fusion.3) | copy-start | bytes 4300804
  139.7 8.1 %collective-permute-start.2 = (f32[20,6,128]{2,1,0:T(8,128)S(1)}, f32[20,6,128]{2,1,0:T(8,128)S(1)}, u32[]{:S(2)}, u32[]{:S(2)}) collective-permute-start(f32[20,6,128]{2,1,0:T(8,128)S(1)} %get-tuple-element.46), channel_id=1, source_target_pairs={{0,1},{1,2},{2,3},{3,0},{4,5},{5,6},{6,7},{7,4},{8,9},{9,10},{10,1... | collective-permute-start | bytes 184328 | tf_op jit(solution)/shard_map/ppermute | solution.py:23
  144.2 4.9 %collective-permute-start.11 = (f32[20,6,128]{2,1,0:T(8,128)S(1)}, f32[20,6,128]{2,1,0:T(8,128)S(1)}, u32[]{:S(2)}, u32[]{:S(2)}) collective-permute-start(f32[20,6,128]{2,1,0:T(8,128)S(1)} %get-tuple-element.49), channel_id=1, source_target_pairs={{1,0},{2,1},{3,2},{0,3},{5,4},{6,5},{7,6},{4,7},{9,8},{10,9},{11,1... | collective-permute-start | bytes 184328 | tf_op jit(solution)/shard_map/ppermute | solution.py:24
  145.6 6.3 %copy-start.14 = (f32[20,128,128]{2,1,0:T(8,128)S(1)}, f32[20,128,128]{2,1,0:T(8,128)}, u32[]{:S(2)}) copy-start(f32[20,128,128]{2,1,0:T(8,128)} %constant_dynamic-update-slice_fusion.6) | copy-start | bytes 3932164
  145.6 6.3 %collective-permute-start.10 = (f32[20,6,128]{2,1,0:T(8,128)S(1)}, f32[20,6,128]{2,1,0:T(8,128)S(1)}, u32[]{:S(2)}, u32[]{:S(2)}) collective-permute-start(f32[20,6,128]{2,1,0:T(8,128)S(1)} %get-tuple-element.48), channel_id=1, source_target_pairs={{0,1},{1,2},{2,3},{3,0},{4,5},{5,6},{6,7},{7,4},{8,9},{9,10},{10,1... | collective-permute-start | bytes 184328 | tf_op jit(solution)/shard_map/ppermute | solution.py:23
  (24 other events, 50.7 us)
where the time goes:
time: 180 us; the launch traced here: 179 us
  blocking collectives  44.2 us (25%)
  local copies, waits for them, and re-layouts  39.7 us (22%)
  other arithmetic  39.6 us (22%)
  starting transfers between devices  24.3 us (14%)
  waiting for transfers between devices  18.4 us (10%)
  matrix products  11.8 us (7%)
    psum x1, blocking collectives, level_means(): lax.psum((jnp.sum(percent, axis=(0, 1)), jnp.sum(theta_out, axis=(0, 1)))...  44.2 us
    ppermute x10, starting transfers between devices, padded_2(): after = lax.ppermute(initial, axis, down)  19.1 us
    another operation x3, other arithmetic, column_tables(): factor = jnp.linalg.cholesky(matrix)  12.4 us
    unnamed x84, local copies, waits for them, and re-layouts  11.7 us
    another operation x2, other arithmetic, column_tables(): lax.linalg.triangular_solve(factor, halfway, left_side=True, lower=True,...  10.5 us
    ppermute x10, waiting for transfers between devices, padded_2(): before = lax.ppermute(last, axis, up)  10.3 us
    ppermute x10, waiting for transfers between devices, padded_2(): after = lax.ppermute(initial, axis, down)  8.11 us
    concatenate x5, local copies, waits for them, and re-layouts, padded_2(): value = jnp.concatenate([before, value, after], axis=dim)  7.08 us
  transfers between devices with their start and end apart: 20, of which 6 were waited for; matrix products, arithmetic and copies ran while one was open for 32% of the time, Pallas kernels for 0%

commit v1 on v0

--- a/solution.py
+++ b/solution.py
@@ -110,9 +110,8 @@
 
 
 def level_means(percent, theta_out, columns):
-    totals = lax.psum(
-        (jnp.sum(percent, axis=(0, 1)), jnp.sum(theta_out, axis=(0, 1))), ("gx", "gy")
-    )
+    u_in = (jnp.sum(percent, axis=(0, 1)), jnp.sum(theta_out, axis=(0, 1)))
+    totals = jax.lax.psum(jax.lax.psum(u_in, "gy"), "gx")
     return (totals[0] / columns, totals[1] / columns)
 
 

time: 180 us -> 158 us (0.88)
  blocking collectives: 44.2 us -> 24.9 us
  starting transfers between devices: 24.3 us -> 21.9 us
    psum x1 -> x2, blocking collectives: 44.2 us -> 24.9 us  [level_means(): totals = jax.lax.psum(jax.lax.psum(u_in, 'gy'), 'gx')]
    ppermute x10, starting transfers between devices: 19.1 us -> 14.6 us  [padded_2(): after = lax.ppermute(initial, axis, down)]
    ppermute x10, starting transfers between devices: 5.2 us -> 7.3 us  [padded_2(): before = lax.ppermute(last, axis, up)]
  transfers between devices with their start and end apart: 20 -> 20, of which waited for: 6 -> 6; matrix products, arithmetic and copies ran while one was open for 32% -> 37% of each run, Pallas kernels for 0% -> 0%
where the time goes in v1:
time: 158 us; the launch traced here: 157 us
  other arithmetic  39.6 us (25%)
  local copies, waits for them, and re-layouts  39.5 us (25%)
  blocking collectives  24.9 us (16%)
  starting transfers between devices  21.9 us (14%)
  waiting for transfers between devices  18.2 us (12%)
  matrix products  11.8 us (7%)
    psum x2, blocking collectives, level_means(): totals = jax.lax.psum(jax.lax.psum(u_in, 'gy'), 'gx')  24.9 us
    ppermute x10, starting transfers between devices, padded_2(): after = lax.ppermute(initial, axis, down)  14.6 us
    another operation x3, other arithmetic, column_tables(): factor = jnp.linalg.cholesky(matrix)  12.4 us
    unnamed x84, local copies, waits for them, and re-layouts  11.6 us
    another operation x2, other arithmetic, column_tables(): lax.linalg.triangular_solve(factor, halfway, left_side=True, lower=True,...  10.5 us
    ppermute x10, waiting for transfers between devices, padded_2(): before = lax.ppermute(last, axis, up)  10 us
    ppermute x10, waiting for transfers between devices, padded_2(): after = lax.ppermute(initial, axis, down)  8.22 us
    ppermute x10, starting transfers between devices, padded_2(): before = lax.ppermute(last, axis, up)  7.3 us
  transfers between devices with their start and end apart: 20, of which 6 were waited for; matrix products, arithmetic and copies ran while one was open for 37% of the time, Pallas kernels for 0%

profile of v1, /device:TPU:0, one launch (start us, length us, event | category | flops | bytes accessed | tf_op | source)
XLA Modules:
  0.0 157.4 jit_solution(10110719615626195086)
XLA Ops:
  0.7 2.1 %fusion.102 = (f32[6,128,128]{2,1,0:T(8,128)}, f32[6,128,128]{2,1,0:T(8,128)}) fusion(f32[8,128,128]{2,1,0:T(8,128)} %param.13), kind=kLoop, calls=%fused_computation.159 | loop fusion | bytes 1572864 | tf_op jit(solution)/shard_map/slice | solution.py:22
  3.3 2.9 %collective-permute-start.5 = (f32[6,128,128]{2,1,0:T(8,128)}, f32[6,128,128]{2,1,0:T(8,128)}, u32[]{:S(2)}, u32[]{:S(2)}) collective-permute-start(f32[6,128,128]{2,1,0:T(8,128)} %get-tuple-element.69), channel_id=1, source_target_pairs={{4,0},{8,4},{12,8},{16,12},{20,16},{24,20},{28,24},{0,28},{5,1},{9... | collective-permute-start | bytes 1179656 | tf_op jit(solution)/shard_map/ppermute | solution.py:24
  7.2 2.6 %collective-permute-start.1 = (f32[6,128,128]{2,1,0:T(8,128)}, f32[6,128,128]{2,1,0:T(8,128)}, u32[]{:S(2)}, u32[]{:S(2)}) collective-permute-start(f32[6,128,128]{2,1,0:T(8,128)} %get-tuple-element.65), channel_id=1, source_target_pairs={{4,0},{8,4},{12,8},{16,12},{20,16},{24,20},{28,24},{0,28},{5,1},{9... | collective-permute-start | bytes 1179656 | tf_op jit(solution)/shard_map/ppermute | solution.py:24
  11.5 4.9 %fusion.6 = (f32[64,8,8,128]{3,2,1,0:T(8,128)}, f32[8,8,128]{2,1,0:T(8,128)S(1)}) fusion(f32[64,8,8,128]{3,2,1,0:T(8,128)} %param.17, f32[8,8,128]{2,1,0:T(8,128)S(1)} %fusion.58, s32[8,8,128]{2,1,0:T(8,128)S(1)} %copy-done.26, bf16[64,8,8,128]{3,2,1,0:T(8,128)(2,1)} %param.18), kind=kLoop, calls=%fused_computation.13 | loop fusion | flops 5758976 | bytes 5341184 | tf_op jit(solution)/shard_map/jit(_where)/select_n | solution.py:107
  17.4 12.7 %all-reduce.2 = (f32[128]{0:T(128)S(1)}, f32[128]{0:T(128)S(1)}) all-reduce(f32[128]{0:T(128)S(1)} %get-tuple-element.33, f32[128]{0:T(128)S(1)} %get-tuple-element.32), channel_id=1, replica_groups=mesh['gx'=8,'gy'=4] {'gy'}, use_global_device_ids=true, to_apply=%region_2.3 | all-reduce | flops 256 | bytes 2048 | tf_op jit(solution)/shard_map/psum | solution.py:114
  30.2 12.2 %all-reduce.1 = (f32[128]{0:T(128)S(1)}, f32[128]{0:T(128)S(1)}) all-reduce(f32[128]{0:T(128)S(1)} %get-tuple-element.36, f32[128]{0:T(128)S(1)} %get-tuple-element.37), channel_id=1, replica_groups=mesh['gx'=8,'gy'=4] {'gx'}, use_global_device_ids=true, to_apply=%region_3.4 | all-reduce | flops 256 | bytes 2048 | tf_op jit(solution)/shard_map/psum | solution.py:114
  44.6 11.7 %cholesky.17 = f32[128,128]{1,0:T(8,128)S(1)} custom-call(f32[128,128]{1,0:T(8,128)S(1)} %fusion.42), custom_call_target="Cholesky" | custom-call | tf_op jit(solution)/shard_map/jit(cholesky)/cholesky | solution.py:43
  57.6 9.8 %custom-call.8 = f32[1,128,128]{1,2,0:T(8,128)S(1)} custom-call(f32[1,128,128]{2,1,0:T(8,128)S(1)} %fusion.36), custom_call_target="InvertDiagBlocksLowerTriangular" | custom-call | tf_op jit(solution)/shard_map/triangular_solve | solution.py:46
  74.7 2.2 %collective-permute-start.9 = (f32[6,128,128]{2,1,0:T(8,128)}, f32[6,128,128]{2,1,0:T(8,128)}, u32[]{:S(2)}, u32[]{:S(2)}) collective-permute-start(f32[6,128,128]{2,1,0:T(8,128)} %get-tuple-element.67), channel_id=1, source_target_pairs={{4,0},{8,4},{12,8},{16,12},{20,16},{24,20},{28,24},{0,28},{5,1},{9... | collective-permute-start | bytes 1179656 | tf_op jit(solution)/shard_map/ppermute | solution.py:24
  78.0 4.7 %collective-permute-done.17 = f32[6,128,128]{1,0,2:T(8,128)S(1)} collective-permute-done((f32[6,128,128]{1,0,2:T(8,128)S(1)}, f32[6,128,128]{1,0,2:T(8,128)S(1)}, u32[]{:S(2)}, u32[]{:S(2)}) %collective-permute-start.17) | collective-permute-done | bytes 393248 | tf_op jit(solution)/shard_map/ppermute | solution.py:24
  82.7 2.8 %collective-permute-start.13 = (f32[6,128,128]{2,0,1:T(8,128)}, f32[6,128,128]{2,0,1:T(8,128)}, u32[]{:S(2)}, u32[]{:S(2)}) collective-permute-start(f32[6,128,128]{2,0,1:T(8,128)} %get-tuple-element.62), channel_id=1, source_target_pairs={{4,0},{8,4},{12,8},{16,12},{20,16},{24,20},{28,24},{0,28},{5,1},{9... | collective-permute-start | bytes 1179656 | tf_op jit(solution)/shard_map/ppermute | solution.py:24
  85.5 2.7 %collective-permute-done.16 = f32[6,128,128]{1,0,2:T(8,128)S(1)} collective-permute-done((f32[6,128,128]{1,0,2:T(8,128)S(1)}, f32[6,128,128]{1,0,2:T(8,128)S(1)}, u32[]{:S(2)}, u32[]{:S(2)}) %collective-permute-start.16) | collective-permute-done | bytes 393248 | tf_op jit(solution)/shard_map/ppermute | solution.py:23
  89.6 2.1 %fusion.94 = (f32[20,6,128]{1,0,2:T(8,128)}, f32[20,6,128]{1,0,2:T(8,128)}) fusion(f32[20,128,128]{1,0,2:T(8,128)S(1)} %pad_maximum_fusion.1), kind=kLoop, calls=%fused_computation.151 | loop fusion | bytes 245760 | tf_op jit(solution)/shard_map/slice | solution.py:21
  91.8 2.0 %collective-permute-start.6 = (f32[20,6,128]{2,1,0:T(8,128)S(1)}, f32[20,6,128]{2,1,0:T(8,128)S(1)}, u32[]{:S(2)}, u32[]{:S(2)}) collective-permute-start(f32[20,6,128]{2,1,0:T(8,128)S(1)} %get-tuple-element.52), channel_id=1, source_target_pairs={{0,1},{1,2},{2,3},{3,0},{4,5},{5,6},{6,7},{7,4},{8,9},{9,10},{10,1... | collective-permute-start | bytes 184328 | tf_op jit(solution)/shard_map/ppermute | solution.py:23
  96.9 1.9 %copy.56 = f32[20,6,128]{2,0,1:T(8,128)S(1)} copy(f32[20,6,128]{1,0,2:T(8,128)} %get-tuple-element.45) | data formatting | bytes 122880 | tf_op jit(solution)/shard_map/slice | solution.py:22
  98.8 1.9 %copy.55 = f32[20,6,128]{2,0,1:T(8,128)S(1)} copy(f32[20,6,128]{1,0,2:T(8,128)} %get-tuple-element.44) | data formatting | bytes 122880 | tf_op jit(solution)/shard_map/slice | solution.py:21
  100.7 1.9 %collective-permute-start.3 = (f32[20,6,128]{2,1,0:T(8,128)S(1)}, f32[20,6,128]{2,1,0:T(8,128)S(1)}, u32[]{:S(2)}, u32[]{:S(2)}) collective-permute-start(f32[20,6,128]{2,1,0:T(8,128)S(1)} %get-tuple-element.49), channel_id=1, source_target_pairs={{1,0},{2,1},{3,2},{0,3},{5,4},{6,5},{7,6},{4,7},{9,8},{10,9},{11,1... | collective-permute-start | bytes 184328 | tf_op jit(solution)/shard_map/ppermute | solution.py:24
  102.6 1.8 %constant_dynamic-update-slice_fusion.6 = f32[20,128,128]{2,1,0:T(8,128)} fusion(f32[20,128,128]{2,1,0:T(8,128)} %copy-done.13, f32[6,128,128]{2,1,0:T(8,128)} %collective-permute-done.9), kind=kLoop, calls=%fused_computation.130 | loop fusion | bytes 786432 | tf_op jit(solution)/shard_map/concatenate | solution.py:25
  105.4 2.0 %collective-permute-start.18 = (f32[20,6,128]{2,0,1:T(8,128)S(1)}, f32[20,6,128]{2,0,1:T(8,128)S(1)}, u32[]{:S(2)}, u32[]{:S(2)}) collective-permute-start(f32[20,6,128]{2,0,1:T(8,128)S(1)} %copy.55), channel_id=1, source_target_pairs={{0,1},{1,2},{2,3},{3,0},{4,5},{5,6},{6,7},{7,4},{8,9},{9,10},{10,1... | collective-permute-start | bytes 184328 | tf_op jit(solution)/shard_map/ppermute | solution.py:23
  110.0 1.5 copy.58
  111.6 1.8 %copy.50 = f32[20,128,128]{2,1,0:T(8,128)S(1)} copy(f32[20,128,128]{2,0,1:T(8,128)} %copy-done.6) | data formatting | bytes 2621440 | tf_op jit(solution)/shard_map/concatenate | solution.py:25
  113.3 1.9 %collective-permute-start.15 = (f32[20,6,128]{2,0,1:T(8,128)S(1)}, f32[20,6,128]{2,0,1:T(8,128)S(1)}, u32[]{:S(2)}, u32[]{:S(2)}) collective-permute-start(f32[20,6,128]{2,0,1:T(8,128)S(1)} %get-tuple-element.43), channel_id=1, source_target_pairs={{1,0},{2,1},{3,2},{0,3},{5,4},{6,5},{7,6},{4,7},{9,8},{10,9},{11,1... | collective-permute-start | bytes 184328 | tf_op jit(solution)/shard_map/ppermute | solution.py:24
  115.7 2.2 %collective-permute-done.15 = f32[20,6,128]{2,0,1:T(8,128)S(1)} collective-permute-done((f32[20,6,128]{2,0,1:T(8,128)S(1)}, f32[20,6,128]{2,0,1:T(8,128)S(1)}, u32[]{:S(2)}, u32[]{:S(2)}) %collective-permute-start.15) | collective-permute-done | bytes 61472 | tf_op jit(solution)/shard_map/ppermute | solution.py:24
  118.0 4.5 %collective-permute-done.14 = f32[20,6,128]{2,0,1:T(8,128)S(1)} collective-permute-done((f32[20,6,128]{2,0,1:T(8,128)S(1)}, f32[20,6,128]{2,0,1:T(8,128)S(1)}, u32[]{:S(2)}, u32[]{:S(2)}) %collective-permute-start.14) | collective-permute-done | bytes 61472 | tf_op jit(solution)/shard_map/ppermute | solution.py:23
  123.8 2.1 %collective-permute-start.10 = (f32[20,6,128]{2,1,0:T(8,128)S(1)}, f32[20,6,128]{2,1,0:T(8,128)S(1)}, u32[]{:S(2)}, u32[]{:S(2)}) collective-permute-start(f32[20,6,128]{2,1,0:T(8,128)S(1)} %get-tuple-element.50), channel_id=1, source_target_pairs={{0,1},{1,2},{2,3},{3,0},{4,5},{5,6},{6,7},{7,4},{8,9},{9,10},{10,1... | collective-permute-start | bytes 184328 | tf_op jit(solution)/shard_map/ppermute | solution.py:23
  127.3 2.8 %collective-permute-done.10 = f32[20,6,128]{2,1,0:T(8,128)S(1)} collective-permute-done((f32[20,6,128]{2,1,0:T(8,128)S(1)}, f32[20,6,128]{2,1,0:T(8,128)S(1)}, u32[]{:S(2)}, u32[]{:S(2)}) %collective-permute-start.10) | collective-permute-done | bytes 61472 | tf_op jit(solution)/shard_map/ppermute | solution.py:23
  135.2 2.1 %reshape.77 = f32[1584,128]{1,0:T(8,128)} reshape(f32[12,132,128]{2,1,0:T(8,128)} %fusion.23) | data formatting | bytes 1622016 | tf_op jit(solution)/shard_map/reshape | solution.py:61
  137.3 2.3 %fusion.21 = f32[12,132,128]{2,1,0:T(8,128)} fusion(f32[20,140,128]{2,1,0:T(8,128)} %copy-done.2, f32[16,136,128]{2,1,0:T(8,128)S(1)} %bitcast.50, f32[128]{0:T(128)S(1)} %fusion.81), kind=kLoop, calls=%fused_computation.50 | loop fusion | flops 608256 | bytes 2433536 | tf_op jit(solution)/shard_map/mul | solution.py:60
  139.5 2.2 %reshape.79 = f32[1584,128]{1,0:T(8,128)} reshape(f32[12,132,128]{2,1,0:T(8,128)} %fusion.21) | data formatting | bytes 1622016 | tf_op jit(solution)/shard_map/reshape | solution.py:60
  141.7 1.9 %fusion.104 = f32[1584,128]{1,0:T(8,128)S(1)} fusion(f32[1584,128]{1,0:T(8,128)} %reshape.79, f32[128,128]{1,0:T(8,128)S(1)} %fusion.37), kind=kOutput, calls=%fused_computation.161 | convolution fusion | flops 311427072 | bytes 1687552 | tf_op jit(solution)/shard_map/dot_general | solution.py:62
  145.4 1.8 %fusion.1 = f32[1584,128]{1,0:T(8,128)} fusion(f32[1584,128]{1,0:T(8,128)S(1)} %copy-done.4, f32[1584,128]{1,0:T(8,128)S(1)} %convolution_subtract_fusion.1, f32[128]{0:T(128)S(1)} %copy-done.27, s32[128]{0:T(128)S(1)} %iota_add_fusion, pred[128]{0:T(512)(128)(4,1)S(1)} %iota_compare_fusion.6), kind=kOutput, calls=%fused_computation.6 | convolution fusion | flops 311947264 | bytes 2434176 | tf_op jit(solution)/shard_map/dot_general | solution.py:68
  147.2 2.1 %reshape.81 = f32[12,132,128]{2,1,0:T(8,128)} reshape(f32[1584,128]{1,0:T(8,128)} %copy-done.5) | data formatting | bytes 1622016 | tf_op jit(solution)/shard_map/reshape | solution.py:72
  (163 shorter events, 41.9 us)
Async XLA Ops:
  0.6 9.2 %copy-start.10 = (f32[8,128,128]{2,1,0:T(8,128)S(1)}, f32[8,128,128]{2,1,0:T(8,128)}, u32[]{:S(2)}) copy-start(f32[8,128,128]{2,1,0:T(8,128)} %param.11) | copy-start | bytes 1572868
  2.8 69.0 %collective-permute-start.4 = (f32[6,128,128]{2,1,0:T(8,128)}, f32[6,128,128]{2,1,0:T(8,128)}, u32[]{:S(2)}, u32[]{:S(2)}) collective-permute-start(f32[6,128,128]{2,1,0:T(8,128)} %get-tuple-element.70), channel_id=1, source_target_pairs={{0,4},{4,8},{8,12},{12,16},{16,20},{20,24},{24,28},{28,0},{1,5},{5... | collective-permute-start | bytes 1179656 | tf_op jit(solution)/shard_map/ppermute | solution.py:23
  3.3 7.5 %copy-start.21 = (f32[8,128,128]{2,1,0:T(8,128)S(1)}, f32[8,128,128]{2,1,0:T(8,128)}, u32[]{:S(2)}) copy-start(f32[8,128,128]{2,1,0:T(8,128)} %param.15) | copy-start | bytes 1572868
  3.3 71.4 %collective-permute-start.5 = (f32[6,128,128]{2,1,0:T(8,128)}, f32[6,128,128]{2,1,0:T(8,128)}, u32[]{:S(2)}, u32[]{:S(2)}) collective-permute-start(f32[6,128,128]{2,1,0:T(8,128)} %get-tuple-element.69), channel_id=1, source_target_pairs={{4,0},{8,4},{12,8},{16,12},{20,16},{24,20},{28,24},{0,28},{5,1},{9... | collective-permute-start | bytes 1179656 | tf_op jit(solution)/shard_map/ppermute | solution.py:24
  7.2 65.9 %collective-permute-start = (f32[6,128,128]{2,1,0:T(8,128)}, f32[6,128,128]{2,1,0:T(8,128)}, u32[]{:S(2)}, u32[]{:S(2)}) collective-permute-start(f32[6,128,128]{2,1,0:T(8,128)} %get-tuple-element.66), channel_id=1, source_target_pairs={{0,4},{4,8},{8,12},{12,16},{16,20},{20,24},{24,28},{28,0},{1,5},{5... | collective-permute-start | bytes 1179656 | tf_op jit(solution)/shard_map/ppermute | solution.py:23
  7.2 84.6 %collective-permute-start.1 = (f32[6,128,128]{2,1,0:T(8,128)}, f32[6,128,128]{2,1,0:T(8,128)}, u32[]{:S(2)}, u32[]{:S(2)}) collective-permute-start(f32[6,128,128]{2,1,0:T(8,128)} %get-tuple-element.65), channel_id=1, source_target_pairs={{4,0},{8,4},{12,8},{16,12},{20,16},{24,20},{28,24},{0,28},{5,1},{9... | collective-permute-start | bytes 1179656 | tf_op jit(solution)/shard_map/ppermute | solution.py:24
  10.8 77.7 %collective-permute-start.8 = (f32[6,128,128]{2,1,0:T(8,128)}, f32[6,128,128]{2,1,0:T(8,128)}, u32[]{:S(2)}, u32[]{:S(2)}) collective-permute-start(f32[6,128,128]{2,1,0:T(8,128)} %get-tuple-element.68), channel_id=1, source_target_pairs={{0,4},{4,8},{8,12},{12,16},{16,20},{20,24},{24,28},{28,0},{1,5},{5... | collective-permute-start | bytes 1179656 | tf_op jit(solution)/shard_map/ppermute | solution.py:23
  10.8 133.7 %copy-start.28 = (s32[128]{0:T(128)}, s32[128]{0:T(128)S(1)}, u32[]{:S(2)}) copy-start(s32[128]{0:T(128)S(1)} %iota_add_fusion) | copy-start | bytes 1540
  10.8 133.7 %copy-start.30 = (pred[128]{0:T(512)(128)(4,1)}, pred[128]{0:T(512)(128)(4,1)S(1)}, u32[]{:S(2)}) copy-start(pred[128]{0:T(512)(128)(4,1)S(1)} %iota_compare_fusion.6) | copy-start | bytes 388
  17.4 50.9 %copy-start = (f32[8,128,128]{1,0,2:T(8,128)}, f32[8,128,128]{1,0,2:T(8,128)S(1)}, u32[]{:S(2)}) copy-start(f32[8,128,128]{1,0,2:T(8,128)S(1)} %get-tuple-element.39) | copy-start | bytes 1572868
  44.1 25.2 %copy-start.23 = (f32[8,128,128]{2,1,0:T(8,128)S(1)}, f32[8,128,128]{2,1,0:T(8,128)}, u32[]{:S(2)}) copy-start(f32[8,128,128]{2,1,0:T(8,128)} %param.12) | copy-start | bytes 1572868
  68.3 75.4 %copy-start.19 = (f32[128,128]{1,0:T(8,128)}, f32[128,128]{1,0:T(8,128)S(1)}, u32[]{:S(2)}) copy-start(f32[128,128]{1,0:T(8,128)S(1)} %fusion.44) | copy-start | bytes 196612
  68.3 65.6 %copy-start.34 = (f32[128]{0:T(128)}, f32[128]{0:T(128)S(1)}, u32[]{:S(2)}) copy-start(f32[128]{0:T(128)S(1)} %broadcast_multiply_fusion.2) | copy-start | bytes 1540
  68.3 68.9 %copy-start.32 = (f32[128]{0:T(128)}, f32[128]{0:T(128)S(1)}, u32[]{:S(2)}) copy-start(f32[128]{0:T(128)S(1)} %fusion.81) | copy-start | bytes 1540
  71.9 10.8 %collective-permute-start.17 = (f32[6,128,128]{1,0,2:T(8,128)S(1)}, f32[6,128,128]{1,0,2:T(8,128)S(1)}, u32[]{:S(2)}, u32[]{:S(2)}) collective-permute-start(f32[6,128,128]{1,0,2:T(8,128)S(1)} %copy-done.25), channel_id=1, source_target_pairs={{4,0},{8,4},{12,8},{16,12},{20,16},{24,20},{28,24},{0,28},{5,1},{9... | collective-permute-start | bytes 1179656 | tf_op jit(solution)/shard_map/ppermute | solution.py:24
  73.1 15.2 %collective-permute-start.16 = (f32[6,128,128]{1,0,2:T(8,128)S(1)}, f32[6,128,128]{1,0,2:T(8,128)S(1)}, u32[]{:S(2)}, u32[]{:S(2)}) collective-permute-start(f32[6,128,128]{1,0,2:T(8,128)S(1)} %copy-done.24), channel_id=1, source_target_pairs={{0,4},{4,8},{8,12},{12,16},{16,20},{20,24},{24,28},{28,0},{1,5},{5... | collective-permute-start | bytes 1179656 | tf_op jit(solution)/shard_map/ppermute | solution.py:23
  74.7 26.0 %collective-permute-start.9 = (f32[6,128,128]{2,1,0:T(8,128)}, f32[6,128,128]{2,1,0:T(8,128)}, u32[]{:S(2)}, u32[]{:S(2)}) collective-permute-start(f32[6,128,128]{2,1,0:T(8,128)} %get-tuple-element.67), channel_id=1, source_target_pairs={{4,0},{8,4},{12,8},{16,12},{20,16},{24,20},{28,24},{0,28},{5,1},{9... | collective-permute-start | bytes 1179656 | tf_op jit(solution)/shard_map/ppermute | solution.py:24
  78.0 10.5 %copy-start.11 = (f32[20,128,128]{2,1,0:T(8,128)}, f32[20,128,128]{2,1,0:T(8,128)S(1)}, u32[]{:S(2)}) copy-start(f32[20,128,128]{2,1,0:T(8,128)S(1)} %constant_dynamic-update-slice_fusion.3) | copy-start | bytes 3932164
  82.7 22.6 %collective-permute-start.13 = (f32[6,128,128]{2,0,1:T(8,128)}, f32[6,128,128]{2,0,1:T(8,128)}, u32[]{:S(2)}, u32[]{:S(2)}) collective-permute-start(f32[6,128,128]{2,0,1:T(8,128)} %get-tuple-element.62), channel_id=1, source_target_pairs={{4,0},{8,4},{12,8},{16,12},{20,16},{24,20},{28,24},{0,28},{5,1},{9... | collective-permute-start | bytes 1179656 | tf_op jit(solution)/shard_map/ppermute | solution.py:24
  88.2 17.2 %collective-permute-start.12 = (f32[6,128,128]{2,0,1:T(8,128)}, f32[6,128,128]{2,0,1:T(8,128)}, u32[]{:S(2)}, u32[]{:S(2)}) collective-permute-start(f32[6,128,128]{2,0,1:T(8,128)} %get-tuple-element.61), channel_id=1, source_target_pairs={{0,4},{4,8},{8,12},{12,16},{16,20},{20,24},{24,28},{28,0},{1,5},{5... | collective-permute-start | bytes 1179656 | tf_op jit(solution)/shard_map/ppermute | solution.py:23
  88.5 35.3 %collective-permute-start.7 = (f32[20,6,128]{2,1,0:T(8,128)S(1)}, f32[20,6,128]{2,1,0:T(8,128)S(1)}, u32[]{:S(2)}, u32[]{:S(2)}) collective-permute-start(f32[20,6,128]{2,1,0:T(8,128)S(1)} %get-tuple-element.53), channel_id=1, source_target_pairs={{1,0},{2,1},{3,2},{0,3},{5,4},{6,5},{7,6},{4,7},{9,8},{10,9},{11,1... | collective-permute-start | bytes 184328 | tf_op jit(solution)/shard_map/ppermute | solution.py:24
  91.8 34.1 %collective-permute-start.6 = (f32[20,6,128]{2,1,0:T(8,128)S(1)}, f32[20,6,128]{2,1,0:T(8,128)S(1)}, u32[]{:S(2)}, u32[]{:S(2)}) collective-permute-start(f32[20,6,128]{2,1,0:T(8,128)S(1)} %get-tuple-element.52), channel_id=1, source_target_pairs={{0,1},{1,2},{2,3},{3,0},{4,5},{5,6},{6,7},{7,4},{8,9},{9,10},{10,1... | collective-permute-start | bytes 184328 | tf_op jit(solution)/shard_map/ppermute | solution.py:23
  100.7 25.3 %collective-permute-start.3 = (f32[20,6,128]{2,1,0:T(8,128)S(1)}, f32[20,6,128]{2,1,0:T(8,128)S(1)}, u32[]{:S(2)}, u32[]{:S(2)}) collective-permute-start(f32[20,6,128]{2,1,0:T(8,128)S(1)} %get-tuple-element.49), channel_id=1, source_target_pairs={{1,0},{2,1},{3,2},{0,3},{5,4},{6,5},{7,6},{4,7},{9,8},{10,9},{11,1... | collective-permute-start | bytes 184328 | tf_op jit(solution)/shard_map/ppermute | solution.py:24
  105.4 8.0 %collective-permute-start.19 = (f32[20,6,128]{2,0,1:T(8,128)S(1)}, f32[20,6,128]{2,0,1:T(8,128)S(1)}, u32[]{:S(2)}, u32[]{:S(2)}) collective-permute-start(f32[20,6,128]{2,0,1:T(8,128)S(1)} %copy.56), channel_id=1, source_target_pairs={{1,0},{2,1},{3,2},{0,3},{5,4},{6,5},{7,6},{4,7},{9,8},{10,9},{11,1... | collective-permute-start | bytes 184328 | tf_op jit(solution)/shard_map/ppermute | solution.py:24
  105.4 9.9 %collective-permute-start.18 = (f32[20,6,128]{2,0,1:T(8,128)S(1)}, f32[20,6,128]{2,0,1:T(8,128)S(1)}, u32[]{:S(2)}, u32[]{:S(2)}) collective-permute-start(f32[20,6,128]{2,0,1:T(8,128)S(1)} %copy.55), channel_id=1, source_target_pairs={{0,1},{1,2},{2,3},{3,0},{4,5},{5,6},{6,7},{7,4},{8,9},{9,10},{10,1... | collective-permute-start | bytes 184328 | tf_op jit(solution)/shard_map/ppermute | solution.py:23
  113.3 4.6 %collective-permute-start.15 = (f32[20,6,128]{2,0,1:T(8,128)S(1)}, f32[20,6,128]{2,0,1:T(8,128)S(1)}, u32[]{:S(2)}, u32[]{:S(2)}) collective-permute-start(f32[20,6,128]{2,0,1:T(8,128)S(1)} %get-tuple-element.43), channel_id=1, source_target_pairs={{1,0},{2,1},{3,2},{0,3},{5,4},{6,5},{7,6},{4,7},{9,8},{10,9},{11,1... | collective-permute-start | bytes 184328 | tf_op jit(solution)/shard_map/ppermute | solution.py:24
  115.3 7.1 %collective-permute-start.14 = (f32[20,6,128]{2,0,1:T(8,128)S(1)}, f32[20,6,128]{2,0,1:T(8,128)S(1)}, u32[]{:S(2)}, u32[]{:S(2)}) collective-permute-start(f32[20,6,128]{2,0,1:T(8,128)S(1)} %get-tuple-element.42), channel_id=1, source_target_pairs={{0,1},{1,2},{2,3},{3,0},{4,5},{5,6},{6,7},{7,4},{8,9},{9,10},{10,1... | collective-permute-start | bytes 184328 | tf_op jit(solution)/shard_map/ppermute | solution.py:23
  115.7 7.1 %copy-start.2 = (f32[20,140,128]{2,1,0:T(8,128)}, f32[20,140,128]{2,1,0:T(8,128)S(1)}, u32[]{:S(2)}) copy-start(f32[20,140,128]{2,1,0:T(8,128)S(1)} %pad_maximum_fusion.3) | copy-start | bytes 4300804
  117.9 8.1 %collective-permute-start.2 = (f32[20,6,128]{2,1,0:T(8,128)S(1)}, f32[20,6,128]{2,1,0:T(8,128)S(1)}, u32[]{:S(2)}, u32[]{:S(2)}) collective-permute-start(f32[20,6,128]{2,1,0:T(8,128)S(1)} %get-tuple-element.48), channel_id=1, source_target_pairs={{0,1},{1,2},{2,3},{3,0},{4,5},{5,6},{6,7},{7,4},{8,9},{9,10},{10,1... | collective-permute-start | bytes 184328 | tf_op jit(solution)/shard_map/ppermute | solution.py:23
  122.4 4.8 %collective-permute-start.11 = (f32[20,6,128]{2,1,0:T(8,128)S(1)}, f32[20,6,128]{2,1,0:T(8,128)S(1)}, u32[]{:S(2)}, u32[]{:S(2)}) collective-permute-start(f32[20,6,128]{2,1,0:T(8,128)S(1)} %get-tuple-element.51), channel_id=1, source_target_pairs={{1,0},{2,1},{3,2},{0,3},{5,4},{6,5},{7,6},{4,7},{9,8},{10,9},{11,1... | collective-permute-start | bytes 184328 | tf_op jit(solution)/shard_map/ppermute | solution.py:24
  123.8 6.3 %copy-start.14 = (f32[20,128,128]{2,1,0:T(8,128)S(1)}, f32[20,128,128]{2,1,0:T(8,128)}, u32[]{:S(2)}) copy-start(f32[20,128,128]{2,1,0:T(8,128)} %constant_dynamic-update-slice_fusion.6) | copy-start | bytes 3932164
  123.8 6.3 %collective-permute-start.10 = (f32[20,6,128]{2,1,0:T(8,128)S(1)}, f32[20,6,128]{2,1,0:T(8,128)S(1)}, u32[]{:S(2)}, u32[]{:S(2)}) collective-permute-start(f32[20,6,128]{2,1,0:T(8,128)S(1)} %get-tuple-element.50), channel_id=1, source_target_pairs={{0,1},{1,2},{2,3},{3,0},{4,5},{5,6},{6,7},{7,4},{8,9},{9,10},{10,1... | collective-permute-start | bytes 184328 | tf_op jit(solution)/shard_map/ppermute | solution.py:23
  (24 other events, 49.4 us)
